TPU v7x, 32 devices: a whole 2x2x4 slice. The times are simulated.
32 devices in a mesh: groups: 2 (over x), row: 8 (over z, y), head: 2 (over core).
Axes of the slice: x: 2, y: 2, z: 4, core: 2. Of those that a mesh axis runs over, the one named last changes fastest.
Arguments:
- hidden: bfloat16 [48, 4096], P('groups'), parts along dimension 0, may hold values from -6 to 6
- norm_gain: float32 [4096], replicated, may hold values from 0.1 to 1.9
- w_query: bfloat16 [8, 256, 4096], P('head', 'row'), may hold values from -0.09375 to 0.09375
- w_key: bfloat16 [8, 256, 4096], P('head', 'row'), may hold values from -0.09375 to 0.09375
- w_value: bfloat16 [8, 512, 4096], P('head', 'row'), may hold values from -0.09375 to 0.09375
- w_outgate: bfloat16 [8, 512, 4096], P('head', 'row'), may hold values from -0.09375 to 0.09375
- w_out: bfloat16 [8, 512, 4096], P('head', 'row'), may hold values from -0.125 to 0.125
- w_gates: bfloat16 [2, 8, 4096], P(None, 'head'), may hold values from -0.09375 to 0.09375
- gate_bias: float32 [2, 8], P(None, 'head'), may hold values from -2 to 4
- headnorm_gain: float32 [8, 512], P('head', 'row'), may hold values from 0.1 to 1.9
- final_gain: float32 [4096], replicated, may hold values from 0.1 to 1.9
- w_vocab: bfloat16 [25152, 4096], P(('row', 'head')), may hold values from -39.0625 to 39.0625
- memory: float32 [48, 8, 256, 512], P('groups', 'head', 'row'), parts along dimension 0, may hold values from -6 to 6
- normalizer: float32 [48, 8, 256], P('groups', 'head', 'row'), parts along dimension 0, may hold values from -6 to 6
- stabilizer: float32 [48, 8], P('groups', 'head'), parts along dimension 0, may hold values from -2 to 2
- targets: int32 [48], P('groups'), parts along dimension 0, may hold values from 0 to 25151
Outputs:
- memory_out: float32 [48, 8, 256, 512], P('groups', 'head', 'row'), parts along dimension 0
- normalizer_out: float32 [48, 8, 256], P('groups', 'head', 'row'), parts along dimension 0
- stabilizer_out: float32 [48, 8], P('groups', 'head'), parts along dimension 0
- hidden_out: bfloat16 [48, 4096], P('groups', ('row', 'head')), parts along dimension 0
- log_prob: float32 [48], P('groups'), parts along dimension 0
There are 2 independent parts, one for each index of `groups`. A program takes and returns all parts, laid end to end along the dimension named above; an argument that names none is the same for every part. Nothing has to cross between parts.
All inputs are finite; a program needn't handle non-finite values.
Results may differ from a plain program's by a relative error of at most 0.0035.
The roundings to bfloat16 on the way count: a program that leaves them out, or rounds other values in their place, can miss the bound.
Values may be sent and summed in bfloat16 or wider, within the bound.
A program may use at most 64 MiB of HBM per device.

v0:
```python
import math

import jax
import jax.numpy as jnp
from jax import lax
from jax.sharding import PartitionSpec as P

QK_DIM = 256


epsilon = 1e-06


def joined_2(value, axis, join):
    pieces = jax.tree.map(lambda part: lax.all_gather(part, axis), value)
    head = jax.tree.map(lambda part: part[0], pieces)
    tail = jax.tree.map(lambda part: part[1:], pieces)
    total, _ = lax.scan(lambda total, share: (join(total, share), None), head, tail)
    return total


def rms_round(stream, gain):
    scale = lax.rsqrt(jnp.mean(stream * stream, axis=-1, keepdims=True) + epsilon)
    return (stream * scale * gain).astype(jnp.bfloat16)


def per_device(
    hidden,
    norm_gain,
    w_query,
    w_key,
    w_value,
    w_outgate,
    w_out,
    w_gates,
    gate_bias,
    headnorm_gain,
    final_gain,
    w_vocab,
    memory,
    normalizer,
    stabilizer,
    targets,
):
    value_rows = w_value.shape[1]
    stream = hidden.astype(jnp.float32)
    normed_in = rms_round(stream, norm_gain)

    def project(weights):
        return jnp.einsum("sd,hjd->shj", normed_in, weights, preferred_element_type=jnp.float32)

    queries = project(w_query) / math.sqrt(QK_DIM)
    key_part = project(w_key)
    value_part = project(w_value).astype(jnp.bfloat16)
    outgate_pre = project(w_outgate)
    gate_pre = (
        jnp.einsum("sd,ghd->gsh", normed_in, w_gates, preferred_element_type=jnp.float32)
        + gate_bias[:, None, :]
    )
    log_forget = jax.nn.log_sigmoid(gate_pre[1])
    stabilizer_out = jnp.maximum(log_forget + stabilizer, gate_pre[0])
    decay_rate = jnp.exp(log_forget + stabilizer - stabilizer_out)
    inflow = jnp.exp(gate_pre[0] - stabilizer_out)
    scaled_key = inflow[:, :, None] * key_part
    memory_out = (
        decay_rate[:, :, None, None] * memory
        + scaled_key[:, :, :, None]
        * lax.all_gather(value_part, "row", axis=2, tiled=True).astype(jnp.float32)[:, :, None, :]
    )
    normalizer_out = decay_rate[:, :, None] * normalizer + scaled_key
    partial_readout = jnp.einsum(
        "shj,shje->she", queries, memory_out, precision=lax.Precision.HIGHEST
    )
    readout = lax.psum(partial_readout, "row")
    average = jnp.mean(readout, axis=-1)
    centered_full = readout - average[:, :, None]
    variance = jnp.mean(centered_full * centered_full, axis=-1)
    centered = lax.dynamic_slice_in_dim(
        centered_full, lax.axis_index("row") * value_rows, value_rows, 2
    )
    normed = centered * lax.rsqrt(variance + epsilon)[:, :, None] * headnorm_gain
    gated_out = (jax.nn.sigmoid(outgate_pre) * normed).astype(jnp.bfloat16)
    partial_terms = jnp.einsum("shj,hjd->sd", gated_out, w_out, preferred_element_type=jnp.float32)
    position = lax.axis_index("row") * lax.axis_size("head") + lax.axis_index("head")
    share_width = hidden.shape[1] // (lax.axis_size("row") * lax.axis_size("head"))
    vocab_here = w_vocab.shape[0]
    projection = lax.psum(partial_terms, ("row", "head"))
    new_full = (stream + projection).astype(jnp.bfloat16)
    final_feat = rms_round(new_full.astype(jnp.float32), final_gain)
    logits = jnp.einsum("sd,vd->sv", final_feat, w_vocab, preferred_element_type=jnp.float32)
    hidden_out = lax.dynamic_slice_in_dim(new_full, position * share_width, share_width, 1)
    local_ids = targets - position * vocab_here
    is_target = jnp.arange(vocab_here, dtype=jnp.int32)[None, :] == local_ids[:, None]
    target_term = jnp.sum(jnp.where(is_target, logits, 0.0), axis=-1)
    local_max = jnp.max(logits, axis=-1)
    local_sum = jnp.sum(jnp.exp(logits - local_max[:, None]), axis=-1)

    def combine(earlier, later):
        highest = jnp.maximum(earlier[0], later[0])
        joined = earlier[1] * jnp.exp(earlier[0] - highest) + later[1] * jnp.exp(later[0] - highest)
        return (highest, joined, earlier[2] + later[2])

    highest, exp_total, picked = joined_2(
        (local_max, local_sum, target_term), ("row", "head"), combine
    )
    log_prob = picked - (highest + jnp.log(exp_total))
    return (memory_out, normalizer_out, stabilizer_out, hidden_out, log_prob)


def solution(mesh):
    in_specs = (
        P("groups", None),
        P(),
        P("head", "row", None),
        P("head", "row", None),
        P("head", "row", None),
        P("head", "row", None),
        P("head", "row", None),
        P(None, "head", None),
        P(None, "head"),
        P("head", "row"),
        P(),
        P(("row", "head"), None),
        P("groups", "head", "row", None),
        P("groups", "head", "row"),
        P("groups", "head"),
        P("groups"),
    )
    out_specs = (
        P("groups", "head", "row", None),
        P("groups", "head", "row"),
        P("groups", "head"),
        P("groups", ("row", "head")),
        P("groups"),
    )
    return jax.shard_map(
        per_device, mesh=mesh, in_specs=in_specs, out_specs=out_specs, check_vma=False
    )
```

profile of v0, /device:TPU:0, one launch (start us, length us, event | category | flops | bytes accessed | tf_op | source)
XLA Modules:
  0.0 280.0 jit_solution(1592682969917463788)
XLA Ops:
  7.2 1.2 fusion.17
  8.5 2.7 convolution_convert_fusion
  11.1 0.1 copy.34
  11.3 33.0 %all_gather.21 = bf16[24,4,512]{0,1,2:T(4,128)(2,1)S(1)} all-gather(bf16[24,4,64]{0,1,2:T(4,128)(2,1)S(1)} %copy.34), channel_id=1, replica_groups=mesh['groups'=2,'row'=8,'head'=2] {'row'}, dimensions={2}, use_global_device_ids=true | all-gather | bytes 110592 | tf_op jit(solution)/shard_map/all_gather | solution.py:68
  44.3 0.3 copy.35
  44.7 1.2 fusion.13
  45.9 0.7 subtract_exponential_fusion.1
  46.6 0.1 copy.32
  46.7 2.2 fusion.28
  48.9 2.2 fusion.7
  51.1 3.4 %multiply_add_fusion = f32[24,4,32,512]{3,2,1,0:T(8,128)S(1)} fusion(f32[24,4,32,512]{3,2,1,0:T(8,128)} %param.30, f32[24,4,512]{2,1,0:T(4,128)S(1)} %copy.36, f32[24,4,32]{2,1,0:T(4,128)S(1)} %copy.33, f32[24,4]{1,0:T(8,128)S(1)} %copy.32), kind=kLoop, calls=%fused_computation.10 | loop fusion | flops 4718592 | bytes 12792192 | tf_op jit(solution)/shard_map/add | solution.py:66
  54.5 2.7 copy-done.1
  57.2 3.1 %fusion.26 = f32[24,4,1,512]{3,2,1,0:T(1,128)S(1)} fusion(f32[24,4,32,512]{3,2,1,0:T(8,128)S(1)} %multiply_add_fusion, f32[24,4,32,1]{2,0,1,3:T(8,128)S(1)} %fusion.7), kind=kOutput, calls=%fused_computation.46 | convolution fusion | flops 18874368 | bytes 6500352 | tf_op jit(solution)/shard_map/shj,shje->she/dot_general | solution.py:71
  60.4 0.7 copy.47
  61.2 0.6 copy.38
  61.8 0.6 dynamic-slice
  63.1 70.0 %all-reduce.7.cloned.1.call-done = f32[24,4,512]{2,0,1:T(8,128)} async-done(((f32[24,4,512]{2,0,1:T(8,128)}), f32[24,4,512]{2,0,1:T(8,128)}) %all-reduce.7.cloned.1.call-update) | async-done | bytes 196624 | tf_op jit(solution)/shard_map/psum | solution.py:74
  133.1 1.0 reduce_sum.55
  134.1 1.1 multiply_reduce_fusion
  135.3 3.8 %convolution_bitcast_fusion = f32[24,4096]{1,0:T(8,128)} fusion(bf16[4,64,4096]{2,1,0:T(8,128)(2,1)S(1)} %copy-done, bf16[4,64,4096]{2,1,0:T(8,128)(2,1)} %param.23, f32[24,4,512]{2,0,1:T(8,128)S(1)} %get-tuple-element.86, s32[]{:T(128)S(6)} %select_n.16, f32[4,64]{1,0:T(4,128)S(1)} %copy-done.6, f32[24,4]{0,1:T(4,128)S(1)} %add_rsqrt_fusion, ...), kind=kOutput, calls=%fused_computation.11 | convolution fusion | flops 101099520 | bytes 4854276 | tf_op jit(solution)/shard_map/shj,hjd->sd/dot_general | solution.py:83
  139.1 90.6 %all-reduce.9.cloned.1.call-done = f32[24,4096]{1,0:T(8,128)} async-done(((f32[24,4096]{1,0:T(8,128)}), f32[24,4096]{1,0:T(8,128)}) %all-reduce.9.cloned.1.call-update) | async-done | bytes 393232 | tf_op jit(solution)/shard_map/psum | solution.py:87
  229.6 1.2 fusion.14
  230.8 8.3 %fusion.50 = (f32[24]{0:T(128)S(1)}, f32[24,1572]{1,0:T(8,128)S(1)}) fusion(bf16[1572,4096]{1,0:T(8,128)(2,1)} %param.29, bf16[24,4096]{1,0:T(8,128)(2,1)S(1)} %get-tuple-element.84, f32[4096]{0:T(1024)S(1)} %copy-done.4, f32[24]{0:T(128)S(1)} %add_rsqrt_fusion.1), kind=kOutput, calls=%fused_computation.74 | convolution fusion | flops 309498688 | bytes 13241920 | tf_op jit(solution)/shard_map/sd,vd->sv/dot_general | solution.py:90
  239.1 0.2 dynamic-update-slice
  239.3 0.2 select_reduce_fusion
  239.6 0.2 dynamic-update-slice.1
  239.8 0.2 dynamic-update-slice.2
  240.0 30.9 %all-reduce.3 = (f32[384]{0:T(512)S(1)}, f32[384]{0:T(512)S(1)}, f32[384]{0:T(512)S(1)}) all-reduce(f32[384]{0:T(512)S(1)} %dynamic-update-slice, f32[384]{0:T(512)S(1)} %dynamic-update-slice.1, f32[384]{0:T(512)S(1)} %dynamic-update-slice.2), channel_id=2, replica_groups=mesh['groups'=2,'row'=8,'head'=2] {'row','head'}, use_global_device_ids=true, to_apply=%add | all-reduce | flops 1152 | bytes 9216
  271.2 0.6 constant_dynamic-slice_fusion.3
  271.9 0.1 reshape.56
  272.0 0.6 while.14
  272.7 0.5 add_subtract_fusion
  (55 shorter events, 1.1 us)
Async XLA Ops:
  7.2 128.1 %copy-start = (bf16[4,64,4096]{2,1,0:T(8,128)(2,1)S(1)}, bf16[4,64,4096]{2,1,0:T(8,128)(2,1)}, u32[]{:S(2)}) copy-start(bf16[4,64,4096]{2,1,0:T(8,128)(2,1)} %param.24) | copy-start | bytes 6291460
  7.2 125.9 %all-reduce.7.cloned.1.call-start = ((), (), s32[]{:S(2)}) async-start(), calls=%async_computation | async-start | bytes 393216 | tf_op jit(solution)/shard_map/psum | solution.py:74
  46.6 7.9 %copy-start.5 = (f32[24,4]{0,1:T(4,128)}, f32[24,4]{0,1:T(4,128)S(1)}, u32[]{:S(2)}) copy-start(f32[24,4]{0,1:T(4,128)S(1)} %get-tuple-element.88) | copy-start | bytes 1156
  54.5 2.7 copy-start.1
  57.2 4.6 %copy-start.8 = (u32[32]{0:T(128)S(1)}, u32[32]{0:T(128)}, u32[]{:S(2)}) copy-start(u32[32]{0:T(128)} %constant.57) | copy-start | bytes 388
  57.2 78.0 %copy-start.2 = (bf16[24,4096]{1,0:T(8,128)(2,1)S(1)}, bf16[24,4096]{1,0:T(8,128)(2,1)}, u32[]{:S(2)}) copy-start(bf16[24,4096]{1,0:T(8,128)(2,1)} %param.18) | copy-start | bytes 589828
  57.2 78.0 %copy-start.3 = (f32[4096]{0:T(1024)S(1)}, f32[4096]{0:T(1024)}, u32[]{:S(2)}) copy-start(f32[4096]{0:T(1024)} %param.19) | copy-start | bytes 49156
  57.2 78.1 %copy-start.6 = (f32[4,64]{1,0:T(4,128)S(1)}, f32[4,64]{1,0:T(4,128)}, u32[]{:S(2)}) copy-start(f32[4,64]{1,0:T(4,128)} %param.27) | copy-start | bytes 3076
  57.2 81.8 %copy-start.7 = (s32[24]{0:T(128)S(1)}, s32[24]{0:T(128)}, u32[]{:S(2)}) copy-start(s32[24]{0:T(128)} %param.33) | copy-start | bytes 292
  57.2 173.6 %copy-start.4 = (f32[4096]{0:T(1024)S(1)}, f32[4096]{0:T(1024)}, u32[]{:S(2)}) copy-start(f32[4096]{0:T(1024)} %param.28) | copy-start | bytes 49156
  61.1 168.5 %all-reduce.9.cloned.1.call-start = ((), (), s32[]{:S(2)}) async-start(), calls=%async_computation.1 | async-start | bytes 786432 | tf_op jit(solution)/shard_map/psum | solution.py:87
Sparse Core Ops, SparseCore 0:
  61.2 71.7 all-reduce.6
  139.2 90.4 all-reduce.8
where the time goes:
time: 281 us; the launch traced here: 280 us
  waiting for transfers between devices  161 us (57%)
  blocking collectives  64 us (23%)
  matrix products  23.4 us (8%)
  between operations  15 us (5%)
  other arithmetic  9.78 us (3%)
  local copies, waits for them, and re-layouts  7.02 us (2%)
    psum x1, waiting for transfers between devices, per_device(): projection = lax.psum(partial_terms, ('row', 'head'))  90.6 us
    psum x1, waiting for transfers between devices, per_device(): readout = lax.psum(partial_readout, 'row')  70 us
    all_gather x1, blocking collectives, per_device(): lax.all_gather(value_part, 'row', axis=2, tiled=True).astype(jnp.float32)  33 us
    unnamed x1, blocking collectives  30.9 us
    dot_general x1, matrix products, per_device(): jnp.einsum('sd,vd->sv', final_feat, w_vocab, preferred_element_type=jnp.f...  8.26 us
    dot_general x3, matrix products, project(): jnp.einsum('sd,hjd->shj', normed_in, weights, preferred_element_type=jnp....  7.03 us
  transfers between devices with their start and end apart: 2, of which 2 were waited for; matrix products, arithmetic and copies ran while one was open for 0% of the time, Pallas kernels for 0%

commit v1 on v0

--- a/solution.py
+++ b/solution.py
@@ -1,14 +1,371 @@
+import functools
 import math
 
 import jax
 import jax.numpy as jnp
 from jax import lax
+from jax.experimental import pallas as pl
+from jax.experimental.pallas import tpu as pltpu
 from jax.sharding import PartitionSpec as P
 
-QK_DIM = 256
-
-
 epsilon = 1e-06
+LANES = 128
+MESH = pl.DeviceIdType.MESH
+
+
+def dot_nt(left, right):
+    return lax.dot_general(left, right, (((1,), (1,)), ((), ())), preferred_element_type=jnp.float32)
+
+
+def lane_of(shape):
+    return lax.broadcasted_iota(jnp.int32, shape, len(shape) - 1)
+
+
+def spread(columns, width, count):
+    head_of = lane_of((columns.shape[0], width * count)) // width
+    total = jnp.zeros((columns.shape[0], width * count), jnp.float32)
+    for h in range(count):
+        total = jnp.where(head_of == h, columns[:, h : h + 1], total)
+    return total
+
+
+def segment_sums(values, width, count):
+    head_of = lane_of(values.shape) // width
+    return [jnp.sum(jnp.where(head_of == h, values, 0.0), axis=-1, keepdims=True) for h in range(count)]
+
+
+def as_rows(columns):
+    seqs = columns[0].shape[0]
+    lane = lane_of((seqs, LANES))
+    wide = jnp.zeros((seqs, LANES), jnp.float32)
+    for i, column in enumerate(columns):
+        wide = jnp.where(lane == i, column, wide)
+    return jnp.transpose(wide)[0:8, :]
+
+
+def kernel(
+    rows, cores, heads,
+    hidden, norm_gain, w_query, w_key, w_value, w_outgate, w_out, w_gates, gate_bias, headnorm, final_gain,
+    w_vocab, memory, stabilizer, targets,
+    values_out, key_out, decay_out, stabilizer_out, hidden_out, log_prob,
+    wq, wk, wv, wg, wo, wvoc, mem,
+    q_cols, part, readout, read_send, read_in, qk_in, stat_in, proj, pair_in, proj_send, proj_in, share, own_share,
+    joined, last_in, small_send,
+    load_sem, v_send, v_recv, qk_send, qk_recv, rd_send, rd_recv, st_send, st_recv,
+    pa_send, pa_recv, pr_send, pr_recv, ag_send, ag_recv, fw_send, fw_recv, ls_send, ls_recv,
+):
+    seqs, model = hidden.shape
+    r = lax.axis_index("row")
+    c = lax.axis_index("head")
+    other = 1 - c
+    spot = r * cores + c
+    keys = w_query.shape[1]
+    vals = w_value.shape[1]
+    head_dim = memory.shape[3]
+    width = share.shape[3]
+
+    loads = [
+        pltpu.make_async_copy(source, target, load_sem.at[i])
+        for i, (source, target) in enumerate(
+            ((w_key, wk), (w_query, wq), (memory, mem), (w_value, wv), (w_outgate, wg), (w_out, wo), (w_vocab, wvoc))
+        )
+    ]
+    for load in loads[:5]:
+        load.start()
+
+    barrier = pltpu.get_barrier_semaphore()
+    for k in range(1, rows * cores):
+        to = lax.rem(spot + k, rows * cores)
+        pl.semaphore_signal(
+            barrier, inc=1, device_id={"row": to // cores, "head": lax.rem(to, cores)}, device_id_type=MESH
+        )
+
+    def to_rows(source_of, target, send, recv):
+        out, back = [], []
+        for k in range(1, rows):
+            to = lax.rem(r + k, rows)
+            come = lax.rem(r + rows - k, rows)
+            where = {"row": to, "head": c}
+            copy = pltpu.make_async_remote_copy(
+                src_ref=source_of(to), dst_ref=target.at[r], send_sem=send.at[k], recv_sem=recv.at[k],
+                device_id=where, device_id_type=MESH,
+            )
+            copy.start()
+            out.append(copy)
+            back.append(
+                pltpu.make_async_remote_copy(
+                    src_ref=source_of(to), dst_ref=target.at[come], send_sem=send.at[k], recv_sem=recv.at[k],
+                    device_id=where, device_id_type=MESH,
+                )
+            )
+        return out, back
+
+    stream = hidden[...].astype(jnp.float32)
+    scale = lax.rsqrt(jnp.mean(stream * stream, axis=-1, keepdims=True) + epsilon)
+    x = (stream * scale * norm_gain[...]).astype(jnp.bfloat16)
+    gate_in = dot_nt(x, w_gates[0]) + gate_bias[0:1, :]
+    gate_forget = dot_nt(x, w_gates[1]) + gate_bias[1:2, :]
+    log_forget = jnp.minimum(gate_forget, 0.0) - jnp.log1p(jnp.exp(-jnp.abs(gate_forget)))
+    top = jnp.maximum(log_forget + stabilizer[...], gate_in)
+    decay = jnp.exp(log_forget + stabilizer[...] - top)
+    inflow = jnp.exp(gate_in - top)
+    stabilizer_out[...] = top
+    decay_out[...] = decay
+
+    loads[0].wait()
+    key = dot_nt(x, wk[...].reshape(heads * keys, model)) * spread(inflow, keys, heads)
+    key_out[...] = key
+    loads[1].wait()
+    query = dot_nt(x, wq[...].reshape(heads * keys, model)) / math.sqrt(rows * keys)
+    query_t = jnp.transpose(query)
+    for s in range(seqs):
+        q_cols[s] = jnp.broadcast_to(query_t[:, s : s + 1], (heads * keys, LANES))
+    small_send[0] = as_rows(segment_sums(query * key, keys, heads))
+    qk_in[r] = small_send[0]
+    pl.semaphore_wait(barrier, rows * cores - 1)
+    qk_out, qk_back = to_rows(lambda to: small_send.at[0], qk_in, qk_send, qk_recv)
+
+    loads[2].wait()
+
+    sublane = lax.broadcasted_iota(jnp.int32, (8, LANES), 0)
+
+    def read(group, carry):
+        for h in range(heads):
+            for t in range(head_dim // LANES):
+                stack = jnp.zeros((8, LANES), jnp.float32)
+                for i in range(8):
+                    s = group * 8 + i
+                    q = q_cols[s, h * keys : (h + 1) * keys, :]
+                    block = mem[s, h, :, t * LANES : (t + 1) * LANES]
+                    stack = jnp.where(sublane == i, jnp.sum(q * block, axis=0, keepdims=True), stack)
+                first = pl.multiple_of(group * 8, 8)
+                readout[h, pl.ds(first, 8), t * LANES : (t + 1) * LANES] = stack
+        return carry
+
+    lax.fori_loop(0, seqs // 8, read, 0)
+    low = lane_of((seqs, LANES)) < vals
+    for pair in range(heads // 2):
+        for t in range(head_dim // LANES):
+            tile = slice(t * LANES, (t + 1) * LANES)
+            a = readout[2 * pair, :, tile] * decay[:, 2 * pair : 2 * pair + 1]
+            b = readout[2 * pair + 1, :, tile] * decay[:, 2 * pair + 1 : 2 * pair + 2]
+            here = slice(pair * LANES, (pair + 1) * LANES)
+            read_send[2 * t, :, here] = jnp.where(low, a, pltpu.roll(b, vals, 1))
+            read_send[2 * t + 1, :, here] = jnp.where(low, pltpu.roll(a, vals, 1), b)
+    read_in[r] = read_send[r]
+    rd_out, rd_back = to_rows(lambda to: read_send.at[to], read_in, rd_send, rd_recv)
+
+    loads[3].wait()
+    value = dot_nt(x, wv[...].reshape(heads * vals, model)).astype(jnp.bfloat16)
+    part[...] = value
+    values_out[r] = value
+    v_out, v_back = to_rows(lambda to: part, values_out, v_send, v_recv)
+    loads[5].start()
+    loads[6].start()
+    loads[4].wait()
+    gate = jax.nn.sigmoid(dot_nt(x, wg[...].reshape(heads * vals, model)))
+
+    for copy in qk_back:
+        copy.wait_recv()
+    qk_rows = qk_in[0]
+    for i in range(1, rows):
+        qk_rows = qk_rows + qk_in[i]
+    qk = jnp.transpose(jnp.concatenate([qk_rows] + [jnp.zeros_like(qk_rows)] * (LANES // 8 - 1), axis=0))
+    value_term = spread(qk, vals, heads) * value.astype(jnp.float32)
+
+    for copy in rd_back:
+        copy.wait_recv()
+    read_full = value_term
+    for i in range(rows):
+        read_full = read_full + read_in[i]
+    means = [total / vals for total in segment_sums(read_full, vals, heads)]
+    local_mean = spread(jnp.concatenate(means, axis=1), vals, heads)
+    offs = read_full - local_mean
+    small_send[1] = as_rows(means + segment_sums(offs * offs, vals, heads))
+    stat_in[r] = small_send[1]
+    st_out, st_back = to_rows(lambda to: small_send.at[1], stat_in, st_send, st_recv)
+    for copy in st_back:
+        copy.wait_recv()
+    average = stat_in[0, 0:heads]
+    spreads = stat_in[0, heads : 2 * heads]
+    for i in range(1, rows):
+        average = average + stat_in[i, 0:heads]
+        spreads = spreads + stat_in[i, heads : 2 * heads]
+    average = average / rows
+    for i in range(rows):
+        off = stat_in[i, 0:heads] - average
+        spreads = spreads + vals * off * off
+    inverse = lax.rsqrt(spreads / head_dim + epsilon)
+    both = jnp.concatenate([average, inverse], axis=0)
+    both = jnp.transpose(jnp.concatenate([both] + [jnp.zeros_like(both)] * (LANES // 8 - 1), axis=0))
+    normed = (read_full - spread(both, vals, heads)) * spread(both[:, heads:], vals, heads) * headnorm[...]
+    gated = (gate * normed).astype(jnp.bfloat16)
+
+    loads[5].wait()
+    for i in range(rows):
+        for j in range(cores):
+            at = (i * cores + j) * width
+            proj[j, i] = jnp.dot(
+                gated, wo[:, :, at : at + width].reshape(heads * vals, width), preferred_element_type=jnp.float32
+            )
+    pair_copy = pltpu.make_async_remote_copy(
+        src_ref=proj.at[other], dst_ref=pair_in, send_sem=pa_send, recv_sem=pa_recv,
+        device_id={"row": r, "head": other}, device_id_type=MESH,
+    )
+    pair_copy.start()
+    pair_copy.wait_recv()
+    for i in range(rows):
+        proj_send[i] = proj[c, i] + pair_in[i]
+    proj_in[r] = proj_send[r]
+    pr_out, pr_back = to_rows(lambda to: proj_send.at[to], proj_in, pr_send, pr_recv)
+    for copy in pr_back:
+        copy.wait_recv()
+    new = proj_in[0]
+    for i in range(1, rows):
+        new = new + proj_in[i]
+    mine = hidden[:, pl.ds(pl.multiple_of(spot * width, LANES), width)].astype(jnp.float32)
+    new = (mine + new).astype(jnp.bfloat16)
+    hidden_out[...] = new
+    own_share[...] = new
+    share[c, r] = new
+    ag_out, ag_back = to_rows(lambda to: own_share, share.at[c], ag_send, ag_recv)
+
+    def forward(source, slot, k):
+        return pltpu.make_async_remote_copy(
+            src_ref=source, dst_ref=share.at[c, slot], send_sem=fw_send.at[k], recv_sem=fw_recv.at[k],
+            device_id={"row": r, "head": other}, device_id_type=MESH,
+        )
+
+    def forwarded(slot, k):
+        return pltpu.make_async_remote_copy(
+            src_ref=own_share, dst_ref=share.at[other, slot], send_sem=fw_send.at[k], recv_sem=fw_recv.at[k],
+            device_id={"row": r, "head": other}, device_id_type=MESH,
+        )
+
+    fw_out, fw_back = [forward(own_share, r, 0)], [forwarded(r, 0)]
+    fw_out[0].start()
+    for k in range(1, rows):
+        ag_back[k - 1].wait_recv()
+        come = lax.rem(r + rows - k, rows)
+        copy = forward(share.at[c, come], come, k)
+        copy.start()
+        fw_out.append(copy)
+        fw_back.append(forwarded(come, k))
+    for copy in fw_back:
+        copy.wait_recv()
+
+    for i in range(rows):
+        for j in range(cores):
+            at = (i * cores + j) * width
+            joined[:, at : at + width] = share[j, i].astype(jnp.float32)
+    full = joined[...]
+    scale = lax.rsqrt(jnp.mean(full * full, axis=-1, keepdims=True) + epsilon)
+    feat = (full * scale * final_gain[...]).astype(jnp.bfloat16)
+    loads[6].wait()
+    vocab_here = w_vocab.shape[0]
+    logits = dot_nt(feat, wvoc[...])
+    entry = lane_of((seqs, vocab_here))
+    picked = jnp.sum(jnp.where(entry == targets[...] - spot * vocab_here, logits, 0.0), axis=-1, keepdims=True)
+    highest = jnp.max(logits, axis=-1, keepdims=True)
+    total = jnp.sum(jnp.exp(logits - highest), axis=-1, keepdims=True)
+    small_send[2] = as_rows([highest, total, picked])
+    last_in[spot] = small_send[2]
+    ls_out, ls_back = [], []
+    for k in range(1, rows * cores):
+        to = lax.rem(spot + k, rows * cores)
+        come = lax.rem(spot + rows * cores - k, rows * cores)
+        for slot, kept in ((spot, ls_out), (come, ls_back)):
+            kept.append(
+                pltpu.make_async_remote_copy(
+                    src_ref=small_send.at[2], dst_ref=last_in.at[slot], send_sem=ls_send.at[k],
+                    recv_sem=ls_recv.at[k], device_id={"row": to // cores, "head": lax.rem(to, cores)},
+                    device_id_type=MESH,
+                )
+            )
+        ls_out[-1].start()
+    for copy in v_back:
+        copy.wait_recv()
+    for copy in ls_back:
+        copy.wait_recv()
+    top = last_in[0, 0:1]
+    for i in range(1, rows * cores):
+        top = jnp.maximum(top, last_in[i, 0:1])
+    total = jnp.zeros_like(top)
+    picked = jnp.zeros_like(top)
+    for i in range(rows * cores):
+        total = total + last_in[i, 1:2] * jnp.exp(last_in[i, 0:1] - top)
+        picked = picked + last_in[i, 2:3]
+    log_prob[...] = picked - (top + jnp.log(total))
+    for copy in qk_out + rd_out + v_out + st_out + [pair_copy] + pr_out + ag_out + fw_out + ls_out:
+        copy.wait_send()
+
+
+def fused(rows, cores, *args):
+    (hidden, norm_gain, w_query, w_key, w_value, w_outgate, w_out, w_gates, gate_bias, headnorm_gain, final_gain,
+     w_vocab, memory, normalizer, stabilizer, targets) = args
+    seqs, model = hidden.shape
+    heads, keys = w_query.shape[:2]
+    vals = w_value.shape[1]
+    head_dim = memory.shape[3]
+    width = model // (rows * cores)
+    f32, bf16 = jnp.float32, jnp.bfloat16
+    vmem = pl.BlockSpec(memory_space=pltpu.VMEM)
+    hbm = pl.BlockSpec(memory_space=pl.ANY)
+    places = [vmem, vmem] + [hbm] * 5 + [vmem] * 4 + [hbm] * 2 + [vmem] * 2
+    dma = pltpu.SemaphoreType.DMA
+    values, key, decay, stabilizer_out, hidden_out, log_prob = pl.pallas_call(
+        functools.partial(kernel, rows, cores, heads),
+        out_shape=[
+            jax.ShapeDtypeStruct((rows, seqs, heads * vals), bf16),
+            jax.ShapeDtypeStruct((seqs, heads * keys), f32),
+            jax.ShapeDtypeStruct((seqs, heads), f32),
+            jax.ShapeDtypeStruct((seqs, heads), f32),
+            jax.ShapeDtypeStruct((seqs, width), bf16),
+            jax.ShapeDtypeStruct((1, seqs), f32),
+        ],
+        in_specs=places,
+        out_specs=[vmem] * 6,
+        scratch_shapes=[
+            pltpu.VMEM(w_query.shape, bf16), pltpu.VMEM(w_key.shape, bf16), pltpu.VMEM(w_value.shape, bf16),
+            pltpu.VMEM(w_outgate.shape, bf16), pltpu.VMEM(w_out.shape, bf16), pltpu.VMEM(w_vocab.shape, bf16),
+            pltpu.VMEM(memory.shape, f32),
+            pltpu.VMEM((seqs, heads * keys, LANES), f32),
+            pltpu.VMEM((seqs, heads * vals), bf16),
+            pltpu.VMEM((heads, seqs, head_dim), f32),
+            pltpu.VMEM((rows, seqs, heads * vals), f32),
+            pltpu.VMEM((rows, seqs, heads * vals), f32),
+            pltpu.VMEM((rows, 8, seqs), f32),
+            pltpu.VMEM((rows, 8, seqs), f32),
+            pltpu.VMEM((cores, rows, seqs, width), f32),
+            pltpu.VMEM((rows, seqs, width), f32),
+            pltpu.VMEM((rows, seqs, width), f32),
+            pltpu.VMEM((rows, seqs, width), f32),
+            pltpu.VMEM((cores, rows, seqs, width), bf16),
+            pltpu.VMEM((seqs, width), bf16),
+            pltpu.VMEM((seqs, model), f32),
+            pltpu.VMEM((rows * cores, 8, seqs), f32),
+            pltpu.VMEM((3, 8, seqs), f32),
+            dma((7,)),
+        ]
+        + [dma((rows,))] * 8
+        + [dma, dma]
+        + [dma((rows,))] * 6
+        + [dma((rows * cores,))] * 2,
+        compiler_params=pltpu.CompilerParams(
+            collective_id=0, has_side_effects=True, vmem_limit_bytes=56 * 1024 * 1024
+        ),
+    )(
+        hidden, norm_gain.reshape(1, model), w_query, w_key, w_value, w_outgate, w_out, w_gates, gate_bias,
+        headnorm_gain.reshape(1, heads * vals), final_gain.reshape(1, model), w_vocab, memory, stabilizer,
+        targets.reshape(seqs, 1),
+    )
+    key = key.reshape(seqs, heads, keys)
+    value = values.reshape(rows, seqs, heads, vals).transpose(1, 2, 0, 3).reshape(seqs, heads, head_dim)
+    memory_out = (
+        decay[:, :, None, None] * memory + key[:, :, :, None] * value.astype(f32)[:, :, None, :]
+    )
+    normalizer_out = decay[:, :, None] * normalizer + key
+    return memory_out, normalizer_out, stabilizer_out, hidden_out, log_prob.reshape(seqs)
 
 
 def joined_2(value, axis, join):
@@ -49,7 +406,7 @@
     def project(weights):
         return jnp.einsum("sd,hjd->shj", normed_in, weights, preferred_element_type=jnp.float32)
 
-    queries = project(w_query) / math.sqrt(QK_DIM)
+    queries = project(w_query) / math.sqrt(w_query.shape[1] * lax.axis_size("row"))
     key_part = project(w_key)
     value_part = project(w_value).astype(jnp.bfloat16)
     outgate_pre = project(w_outgate)
@@ -133,6 +490,14 @@
         P("groups", ("row", "head")),
         P("groups"),
     )
+    rows, cores = mesh.shape["row"], mesh.shape["head"]
+
+    def step(*args):
+        model, heads, vals = args[0].shape[1], args[2].shape[0], args[4].shape[1]
+        lined_up = 2 * vals == LANES and heads % 2 == 0 and 2 * heads <= 8 and cores == 2
+        lined_up = lined_up and args[0].shape[0] % 8 == 0 and heads * args[2].shape[1] == LANES and model % (rows * cores * LANES) == 0
+        return fused(rows, cores, *args) if lined_up else per_device(*args)
+
     return jax.shard_map(
-        per_device, mesh=mesh, in_specs=in_specs, out_specs=out_specs, check_vma=False
-    )
+        step, mesh=mesh, in_specs=in_specs, out_specs=out_specs, check_vma=False
+    )

time: 281 us -> 59.4 us (0.21)
  waiting for transfers between devices: 161 us -> 0 us
  blocking collectives: 64 us -> 0 us
  Pallas kernels: 0 us -> 43.8 us
  matrix products: 23.4 us -> 0 us
  between operations: 15 us -> 0.71 us
  other arithmetic: 9.78 us -> 6.4 us
    psum x2 -> x0, waiting for transfers between devices: 161 us -> none  [the longest x1 90.6 us: per_device(): projection = lax.psum(partial_terms, ('row', 'head'))]
    pallas_call x0 -> x1, Pallas kernels: none -> 43.8 us  [fused(): pl.pallas_call(functools.partial(kernel, rows, cores, heads), out_shape=[...]
    all_gather x1 -> x0, blocking collectives: 33 us -> none  [per_device(): lax.all_gather(value_part, 'row', axis=2, tiled=True).astype(jnp.float32)]
    unnamed x1 -> x0, blocking collectives: 30.9 us -> none
    dot_general x7 -> x0, matrix products: 23.4 us -> none  [the longest x1 8.26 us: per_device(): jnp.einsum('sd,vd->sv', final_feat, w_vocab, preferred_element_type=jnp.f...]
    reduce_sum x5 -> x0, other arithmetic: 4.7 us -> none  [the longest x2 2.38 us: rms_round(): jnp.mean(stream * stream, axis=-1, keepdims=True) + epsilon]
    add x16 -> x2, other arithmetic: 3.81 us -> 6.4 us  [the longest x1 5.69 us: fused(): decay[:, :, None, None] * memory]
  transfers between devices with their start and end apart: 2 -> 0, of which waited for: 2 -> 0; matrix products, arithmetic and copies ran while one was open for 0% -> 0% of each run, Pallas kernels for 0% -> 0%
where the time goes in v1:
time: 59.4 us; the launch traced here: 59.1 us
  Pallas kernels  43.8 us (74%)
  local copies, waits for them, and re-layouts  8.18 us (14%)
  other arithmetic  6.4 us (11%)
  between operations  0.71 us (1%)
    pallas_call x1, Pallas kernels, fused(): pl.pallas_call(functools.partial(kernel, rows, cores, heads), out_shape=[...  43.8 us
    add x1, other arithmetic, fused(): decay[:, :, None, None] * memory  5.69 us
    unnamed x14, local copies, waits for them, and re-layouts  3.15 us
    convert_element_type x4, local copies, waits for them, and re-layouts, fused(): value.astype(f32)[:, :, None, :]  1.59 us
    reshape x1, local copies, waits for them, and re-layouts, fused(): targets.reshape(seqs, 1)  1.33 us
    reshape x1, local copies, waits for them, and re-layouts, fused(): headnorm_gain.reshape(1, heads * vals)  1.32 us

profile of v1, /device:TPU:0, one launch (start us, length us, event | category | flops | bytes accessed | tf_op | source)
XLA Modules:
  0.0 59.1 jit_solution(10465302935734287725)
XLA Ops:
  0.6 1.4 %copy.24.stabilizer = f32[24,4]{1,0:T(8,128)} copy(f32[24,4]{0,1:T(4,128)} %param.30) | data formatting | bytes 768 | tf_op args[14]
  2.0 1.3 %copy.25.targets = s32[24,1]{1,0:T(8,128)} copy(s32[24,1]{0,1:T(1,128)} %bitcast.14) | data formatting | bytes 192 | tf_op jit(solution)/shard_map/reshape | solution.py:360
  3.3 1.3 %reshape.41.headnorm = f32[1,256]{1,0:T(1,128)} reshape(f32[4,64]{1,0:T(4,128)} %param.25) | data formatting | bytes 2048 | tf_op jit(solution)/shard_map/reshape | solution.py:359
  4.6 43.8 %shard_map.191 = (bf16[8,24,256]{2,1,0:T(8,128)(2,1)}, f32[24,128]{1,0:T(8,128)}, f32[24,4]{1,0:T(8,128)}, f32[24,4]{1,0:T(8,128)}, bf16[24,256]{1,0:T(8,128)(2,1)}, /*index=5*/f32[1,24]{1,0:T(1,128)}) custom-call(bf16[24,4096]{1,0:T(8,128)(2,1)} %hidden.1, f32[1,4096]{1,0:T(1,128)} %bitcast.12, bf16[4,32,4096]{2,1,0:T(8,128)(2,1)} %w_query.1, ...), custom_call_target="tpu_custom_call" | custom-call | tf_op jit(solution)/shard_map/pallas_call | solution.py:316
  48.4 0.8 %mul.33 = f32[24,4,32]{2,1,0:T(4,128)S(1)} reshape(f32[24,128]{1,0:T(8,128)} %get-tuple-element.12) | data formatting | bytes 24576 | tf_op jit(solution)/shard_map/mul | solution.py:365
  49.2 1.1 %reshape.46 = f32[8,24,4,64]{3,2,1,0:T(4,128)S(1)} reshape(bf16[8,24,256]{2,1,0:T(8,128)(2,1)} %get-tuple-element.13) | data formatting | bytes 294912 | tf_op jit(solution)/shard_map/convert_element_type | solution.py:365
  50.3 0.2 copy.30
  50.6 0.1 reshape.45
  50.7 0.1 copy.27
  50.8 0.0 copy-start
  50.9 0.0 copy-start.1
  50.9 0.0 copy-start.3
  50.9 0.0 copy-start.2
  50.9 0.0 copy-start.4
  50.9 5.7 %multiply_add_fusion = f32[24,4,32,512]{3,2,1,0:T(8,128)} fusion(f32[24,4,32,512]{3,2,1,0:T(8,128)} %memory.1, f32[24,4,512]{2,1,0:T(4,128)S(1)} %copy.27, f32[24,4,32]{2,1,0:T(4,128)S(1)} %mul.33, f32[24,4]{1,0:T(8,128)} %get-tuple-element.11), kind=kLoop, calls=%fused_computation | loop fusion | flops 4718592 | bytes 12792192 | tf_op jit(solution)/shard_map/add | solution.py:365
  56.6 0.0 copy-done
  56.6 0.0 copy-done.1
  56.6 0.7 %multiply_add_fusion.1 = f32[24,4,32]{2,1,0:T(4,128)} fusion(f32[24,4,32]{2,1,0:T(4,128)S(1)} %mul.33, f32[24,4,32]{2,1,0:T(4,128)S(1)} %copy-done.1, f32[24,4]{1,0:T(8,128)S(1)} %copy-done), kind=kLoop, calls=%fused_computation.2 | loop fusion | flops 6144 | bytes 37248 | tf_op jit(solution)/shard_map/add | solution.py:367
  57.3 0.0 copy-done.3
  57.3 0.7 %copy.28 = f32[24,4]{0,1:T(4,128)} copy(f32[24,4]{1,0:T(8,128)S(1)} %copy-done.3) | data formatting | bytes 768
  58.0 0.0 copy-done.2
  58.0 0.6 %copy.33 = bf16[24,256]{1,0:T(8,128)(2,1)} copy(bf16[24,256]{1,0:T(8,128)(2,1)S(1)} %copy-done.2) | data formatting | bytes 24576
  58.6 0.0 copy-done.4
  58.6 0.5 copy.34
Async XLA Ops:
  50.8 5.7 %copy-start = (f32[24,4]{1,0:T(8,128)S(1)}, f32[24,4]{1,0:T(8,128)}, u32[]{:S(2)}) copy-start(f32[24,4]{1,0:T(8,128)} %get-tuple-element.11) | copy-start | bytes 1156
  50.9 5.7 %copy-start.1 = (f32[24,4,32]{2,1,0:T(4,128)S(1)}, f32[24,4,32]{2,1,0:T(4,128)}, u32[]{:S(2)}) copy-start(f32[24,4,32]{2,1,0:T(4,128)} %param.29) | copy-start | bytes 36868
  50.9 6.4 %copy-start.3 = (f32[24,4]{1,0:T(8,128)S(1)}, f32[24,4]{1,0:T(8,128)}, u32[]{:S(2)}) copy-start(f32[24,4]{1,0:T(8,128)} %get-tuple-element.24) | copy-start | bytes 1156
  50.9 7.1 %copy-start.2 = (bf16[24,256]{1,0:T(8,128)(2,1)S(1)}, bf16[24,256]{1,0:T(8,128)(2,1)}, u32[]{:S(2)}) copy-start(bf16[24,256]{1,0:T(8,128)(2,1)} %get-tuple-element.35) | copy-start | bytes 36868
  50.9 7.7 %copy-start.4 = (f32[1,24]{1,0:T(1,128)S(1)}, f32[1,24]{1,0:T(1,128)}, u32[]{:S(2)}) copy-start(f32[1,24]{1,0:T(1,128)} %get-tuple-element.16) | copy-start | bytes 292

commit v2 on v1

--- a/solution.py
+++ b/solution.py
@@ -46,9 +46,9 @@
 def kernel(
     rows, cores, heads,
     hidden, norm_gain, w_query, w_key, w_value, w_outgate, w_out, w_gates, gate_bias, headnorm, final_gain,
-    w_vocab, memory, stabilizer, targets,
-    values_out, key_out, decay_out, stabilizer_out, hidden_out, log_prob,
-    wq, wk, wv, wg, wo, wvoc, mem,
+    w_vocab, memory, normalizer, stabilizer_t, targets,
+    mem, normalizer_out, stabilizer_out, hidden_out, log_prob,
+    wq, wk, wv, wg, wo, wvoc, values_out, key_cols, decay_rows, value_rows,
     q_cols, part, readout, read_send, read_in, qk_in, stat_in, proj, pair_in, proj_send, proj_in, share, own_share,
     joined, last_in, small_send,
     load_sem, v_send, v_recv, qk_send, qk_recv, rd_send, rd_recv, st_send, st_recv,
@@ -70,8 +70,8 @@
             ((w_key, wk), (w_query, wq), (memory, mem), (w_value, wv), (w_outgate, wg), (w_out, wo), (w_vocab, wvoc))
         )
     ]
-    for load in loads[:5]:
-        load.start()
+    for i in (0, 1, 3, 2, 4):
+        loads[i].start()
 
     barrier = pltpu.get_barrier_semaphore()
     for k in range(1, rows * cores):
@@ -100,30 +100,43 @@
             )
         return out, back
 
+    stabilizer = jnp.transpose(jnp.concatenate([stabilizer_t[...]] * (LANES // heads), axis=0))[:, 0:heads]
+    wanted = jnp.transpose(jnp.broadcast_to(targets[...].astype(jnp.float32), (LANES, seqs)))[:, 0:1].astype(jnp.int32)
+    gain_rows = jnp.concatenate([headnorm[h : h + 1, :] for h in range(heads)], axis=1)
     stream = hidden[...].astype(jnp.float32)
     scale = lax.rsqrt(jnp.mean(stream * stream, axis=-1, keepdims=True) + epsilon)
     x = (stream * scale * norm_gain[...]).astype(jnp.bfloat16)
     gate_in = dot_nt(x, w_gates[0]) + gate_bias[0:1, :]
     gate_forget = dot_nt(x, w_gates[1]) + gate_bias[1:2, :]
     log_forget = jnp.minimum(gate_forget, 0.0) - jnp.log1p(jnp.exp(-jnp.abs(gate_forget)))
-    top = jnp.maximum(log_forget + stabilizer[...], gate_in)
-    decay = jnp.exp(log_forget + stabilizer[...] - top)
+    top = jnp.maximum(log_forget + stabilizer, gate_in)
+    decay = jnp.exp(log_forget + stabilizer - top)
     inflow = jnp.exp(gate_in - top)
-    stabilizer_out[...] = top
-    decay_out[...] = decay
+    stabilizer_out[...] = as_rows([top[:, h : h + 1] for h in range(heads)])[0:heads]
+    for h in range(heads):
+        decay_rows[h] = jnp.broadcast_to(decay[:, h : h + 1], (seqs, LANES))
 
     loads[0].wait()
     key = dot_nt(x, wk[...].reshape(heads * keys, model)) * spread(inflow, keys, heads)
-    key_out[...] = key
+    for h in range(heads):
+        normalizer_out[:, h, :] = decay[:, h : h + 1] * normalizer[:, h, :] + key[:, h * keys : (h + 1) * keys]
+    key_t = jnp.transpose(key)
     loads[1].wait()
     query = dot_nt(x, wq[...].reshape(heads * keys, model)) / math.sqrt(rows * keys)
     query_t = jnp.transpose(query)
     for s in range(seqs):
         q_cols[s] = jnp.broadcast_to(query_t[:, s : s + 1], (heads * keys, LANES))
+        key_cols[s] = jnp.broadcast_to(key_t[:, s : s + 1], (heads * keys, LANES))
     small_send[0] = as_rows(segment_sums(query * key, keys, heads))
     qk_in[r] = small_send[0]
     pl.semaphore_wait(barrier, rows * cores - 1)
     qk_out, qk_back = to_rows(lambda to: small_send.at[0], qk_in, qk_send, qk_recv)
+
+    loads[3].wait()
+    value = dot_nt(x, wv[...].reshape(heads * vals, model)).astype(jnp.bfloat16)
+    part[...] = value
+    values_out[r] = value
+    v_out, v_back = to_rows(lambda to: part, values_out, v_send, v_recv)
 
     loads[2].wait()
 
@@ -155,16 +168,39 @@
     read_in[r] = read_send[r]
     rd_out, rd_back = to_rows(lambda to: read_send.at[to], read_in, rd_send, rd_recv)
 
-    loads[3].wait()
-    value = dot_nt(x, wv[...].reshape(heads * vals, model)).astype(jnp.bfloat16)
-    part[...] = value
-    values_out[r] = value
-    v_out, v_back = to_rows(lambda to: part, values_out, v_send, v_recv)
     loads[5].start()
     loads[6].start()
     loads[4].wait()
     gate = jax.nn.sigmoid(dot_nt(x, wg[...].reshape(heads * vals, model)))
 
+    for copy in v_back:
+        copy.wait_recv()
+    for h in range(heads):
+        here = slice((h // 2) * LANES, (h // 2 + 1) * LANES)
+        for t in range(head_dim // LANES):
+            a = values_out[2 * t, :, here].astype(jnp.float32)
+            b = values_out[2 * t + 1, :, here].astype(jnp.float32)
+            if h % 2:
+                a = pltpu.roll(a, vals, 1)
+            else:
+                b = pltpu.roll(b, vals, 1)
+            value_rows[h, :, t * LANES : (t + 1) * LANES] = jnp.where(low, a, b)
+
+    def update(group, carry):
+        first = pl.multiple_of(group * 8, 8)
+        for h in range(heads):
+            keep = decay_rows[h, pl.ds(first, 8), :]
+            for t in range(head_dim // LANES):
+                tile = slice(t * LANES, (t + 1) * LANES)
+                fresh = value_rows[h, pl.ds(first, 8), tile]
+                for i in range(8):
+                    s = group * 8 + i
+                    old = mem[s, h, :, tile]
+                    column = key_cols[s, h * keys : (h + 1) * keys, :]
+                    mem[s, h, :, tile] = keep[i : i + 1] * old + column * fresh[i : i + 1]
+        return carry
+
+    lax.fori_loop(0, seqs // 8, update, 0)
     for copy in qk_back:
         copy.wait_recv()
     qk_rows = qk_in[0]
@@ -198,7 +234,7 @@
     inverse = lax.rsqrt(spreads / head_dim + epsilon)
     both = jnp.concatenate([average, inverse], axis=0)
     both = jnp.transpose(jnp.concatenate([both] + [jnp.zeros_like(both)] * (LANES // 8 - 1), axis=0))
-    normed = (read_full - spread(both, vals, heads)) * spread(both[:, heads:], vals, heads) * headnorm[...]
+    normed = (read_full - spread(both, vals, heads)) * spread(both[:, heads:], vals, heads) * gain_rows
     gated = (gate * normed).astype(jnp.bfloat16)
 
     loads[5].wait()
@@ -265,7 +301,7 @@
     vocab_here = w_vocab.shape[0]
     logits = dot_nt(feat, wvoc[...])
     entry = lane_of((seqs, vocab_here))
-    picked = jnp.sum(jnp.where(entry == targets[...] - spot * vocab_here, logits, 0.0), axis=-1, keepdims=True)
+    picked = jnp.sum(jnp.where(entry == wanted - spot * vocab_here, logits, 0.0), axis=-1, keepdims=True)
     highest = jnp.max(logits, axis=-1, keepdims=True)
     total = jnp.sum(jnp.exp(logits - highest), axis=-1, keepdims=True)
     small_send[2] = as_rows([highest, total, picked])
@@ -283,8 +319,6 @@
                 )
             )
         ls_out[-1].start()
-    for copy in v_back:
-        copy.wait_recv()
     for copy in ls_back:
         copy.wait_recv()
     top = last_in[0, 0:1]
@@ -311,24 +345,26 @@
     f32, bf16 = jnp.float32, jnp.bfloat16
     vmem = pl.BlockSpec(memory_space=pltpu.VMEM)
     hbm = pl.BlockSpec(memory_space=pl.ANY)
-    places = [vmem, vmem] + [hbm] * 5 + [vmem] * 4 + [hbm] * 2 + [vmem] * 2
+    places = [vmem, vmem] + [hbm] * 5 + [vmem] * 4 + [hbm] * 2 + [vmem] * 3
     dma = pltpu.SemaphoreType.DMA
-    values, key, decay, stabilizer_out, hidden_out, log_prob = pl.pallas_call(
+    memory_out, normalizer_out, stabilizer_out, hidden_out, log_prob = pl.pallas_call(
         functools.partial(kernel, rows, cores, heads),
         out_shape=[
-            jax.ShapeDtypeStruct((rows, seqs, heads * vals), bf16),
-            jax.ShapeDtypeStruct((seqs, heads * keys), f32),
-            jax.ShapeDtypeStruct((seqs, heads), f32),
-            jax.ShapeDtypeStruct((seqs, heads), f32),
+            pltpu.VMEM(memory.shape, f32),
+            jax.ShapeDtypeStruct(normalizer.shape, f32),
+            jax.ShapeDtypeStruct((heads, seqs), f32),
             jax.ShapeDtypeStruct((seqs, width), bf16),
             jax.ShapeDtypeStruct((1, seqs), f32),
         ],
         in_specs=places,
-        out_specs=[vmem] * 6,
+        out_specs=[vmem] * 5,
         scratch_shapes=[
             pltpu.VMEM(w_query.shape, bf16), pltpu.VMEM(w_key.shape, bf16), pltpu.VMEM(w_value.shape, bf16),
             pltpu.VMEM(w_outgate.shape, bf16), pltpu.VMEM(w_out.shape, bf16), pltpu.VMEM(w_vocab.shape, bf16),
-            pltpu.VMEM(memory.shape, f32),
+            pltpu.VMEM((rows, seqs, heads * vals), bf16),
+            pltpu.VMEM((seqs, heads * keys, LANES), f32),
+            pltpu.VMEM((heads, seqs, LANES), f32),
+            pltpu.VMEM((heads, seqs, head_dim), f32),
             pltpu.VMEM((seqs, heads * keys, LANES), f32),
             pltpu.VMEM((seqs, heads * vals), bf16),
             pltpu.VMEM((heads, seqs, head_dim), f32),
@@ -352,20 +388,14 @@
         + [dma((rows,))] * 6
         + [dma((rows * cores,))] * 2,
         compiler_params=pltpu.CompilerParams(
-            collective_id=0, has_side_effects=True, vmem_limit_bytes=56 * 1024 * 1024
+            collective_id=0, has_side_effects=True, vmem_limit_bytes=48 * 1024 * 1024
         ),
     )(
         hidden, norm_gain.reshape(1, model), w_query, w_key, w_value, w_outgate, w_out, w_gates, gate_bias,
-        headnorm_gain.reshape(1, heads * vals), final_gain.reshape(1, model), w_vocab, memory, stabilizer,
-        targets.reshape(seqs, 1),
-    )
-    key = key.reshape(seqs, heads, keys)
-    value = values.reshape(rows, seqs, heads, vals).transpose(1, 2, 0, 3).reshape(seqs, heads, head_dim)
-    memory_out = (
-        decay[:, :, None, None] * memory + key[:, :, :, None] * value.astype(f32)[:, :, None, :]
-    )
-    normalizer_out = decay[:, :, None] * normalizer + key
-    return memory_out, normalizer_out, stabilizer_out, hidden_out, log_prob.reshape(seqs)
+        headnorm_gain, final_gain.reshape(1, model), w_vocab, memory, normalizer, stabilizer.T,
+        targets.reshape(1, seqs),
+    )
+    return memory_out, normalizer_out, stabilizer_out.T, hidden_out, log_prob.reshape(seqs)
 
 
 def joined_2(value, axis, join):

time: 59.4 us -> 49.9 us (0.84)
  other arithmetic: 6.4 us -> 0 us
  local copies, waits for them, and re-layouts: 8.18 us -> 5.03 us
    add x2 -> x0, other arithmetic: 6.4 us -> none  [the longest x1 5.69 us: fused(): decay[:, :, None, None] * memory]
    reshape x2 -> x0, local copies, waits for them, and re-layouts: 2.65 us -> none  [the longest x1 1.33 us: fused(): targets.reshape(seqs, 1)]
    unnamed x14 -> x13, local copies, waits for them, and re-layouts: 3.15 us -> 5.03 us
    convert_element_type x4 -> x0, local copies, waits for them, and re-layouts: 1.59 us -> none  [fused(): value.astype(f32)[:, :, None, :]]
    mul x1 -> x0, local copies, waits for them, and re-layouts: 0.79 us -> none  [fused(): key[:, :, :, None] * value.astype(f32)[:, :, None, :]]
where the time goes in v2:
time: 49.9 us; the launch traced here: 49.8 us
  Pallas kernels  44.1 us (88%)
  local copies, waits for them, and re-layouts  5.03 us (10%)
  between operations  0.68 us (1%)
    pallas_call x1, Pallas kernels, fused(): pl.pallas_call(functools.partial(kernel, rows, cores, heads), out_shape=[...  44.1 us
    unnamed x13, local copies, waits for them, and re-layouts  5.03 us

profile of v2, /device:TPU:0, one launch (start us, length us, event | category | flops | bytes accessed | tf_op | source)
XLA Modules:
  0.0 49.8 jit_solution(10487426843755747464)
XLA Ops:
  0.6 44.1 %shard_map.191 = (f32[24,4,32,512]{3,2,1,0:T(8,128)S(1)}, f32[24,4,32]{2,1,0:T(4,128)}, f32[4,24]{1,0:T(4,128)}, bf16[24,256]{1,0:T(8,128)(2,1)}, f32[1,24]{1,0:T(1,128)}) custom-call(bf16[24,4096]{1,0:T(8,128)(2,1)} %hidden.1, f32[1,4096]{1,0:T(1,128)} %bitcast.6, bf16[4,32,4096]{2,1,0:T(8,128)(2,1)} %w_query.1, bf16[4,32,4096]{2,1,0:T(8,128)(2,1)} %w_key.1, ...), custom_call_target="tpu_custom_call" | custom-call | tf_op jit(solution)/shard_map/pallas_call | solution.py:350
  44.7 0.0 copy-start
  44.7 0.0 copy-start.2
  44.7 0.0 copy-start.1
  44.7 0.0 copy-start.3
  44.8 2.7 %copy.26 = f32[24,4,32,512]{3,2,1,0:T(8,128)} copy(f32[24,4,32,512]{3,2,1,0:T(8,128)S(1)} %get-tuple-element.15) | data formatting | bytes 12582912
  47.5 0.0 copy-done
  47.5 0.6 %copy.27 = f32[24,4,32]{2,1,0:T(4,128)} copy(f32[24,4,32]{2,1,0:T(4,128)S(1)} %copy-done) | data formatting | bytes 24576
  48.1 0.0 copy-done.2
  48.1 0.6 %copy.28 = f32[24,4]{0,1:T(4,128)} copy(f32[24,4]{0,1:T(4,128)S(1)} %bitcast.9) | data formatting | bytes 768
  48.7 0.0 copy-done.1
  48.7 0.6 %copy.29 = bf16[24,256]{1,0:T(8,128)(2,1)} copy(bf16[24,256]{1,0:T(8,128)(2,1)S(1)} %copy-done.1) | data formatting | bytes 24576
  49.3 0.0 copy-done.3
  49.3 0.5 %copy.30 = f32[24]{0:T(128)} copy(f32[24]{0:T(128)S(1)} %bitcast.11) | data formatting | bytes 192
Async XLA Ops:
  44.7 2.7 %copy-start = (f32[24,4,32]{2,1,0:T(4,128)S(1)}, f32[24,4,32]{2,1,0:T(4,128)}, u32[]{:S(2)}) copy-start(f32[24,4,32]{2,1,0:T(4,128)} %get-tuple-element.26) | copy-start | bytes 36868
  44.7 3.4 %copy-start.2 = (f32[4,24]{1,0:T(4,128)S(1)}, f32[4,24]{1,0:T(4,128)}, u32[]{:S(2)}) copy-start(f32[4,24]{1,0:T(4,128)} %get-tuple-element.12) | copy-start | bytes 1156
  44.7 3.9 %copy-start.1 = (bf16[24,256]{1,0:T(8,128)(2,1)S(1)}, bf16[24,256]{1,0:T(8,128)(2,1)}, u32[]{:S(2)}) copy-start(bf16[24,256]{1,0:T(8,128)(2,1)} %get-tuple-element.28) | copy-start | bytes 36868
  44.7 4.5 %copy-start.3 = (f32[1,24]{1,0:T(1,128)S(1)}, f32[1,24]{1,0:T(1,128)}, u32[]{:S(2)}) copy-start(f32[1,24]{1,0:T(1,128)} %get-tuple-element.14) | copy-start | bytes 292
